TPU v7x, 256 devices: a whole 4x4x8 slice. The times are simulated.
256 devices in a mesh: dom: 64 (over z, y, core), sub: 4 (over x).
Axes of the slice: x: 4, y: 4, z: 8, core: 2. Of those that a mesh axis runs over, the one named last changes fastest.
Arguments:
- diag_block: bfloat16 [30, 30, 32768], P(None, None, ('dom', 'sub')), may hold values from -6 to 6
- face_block: bfloat16 [6, 30, 30, 32768], P(None, None, None, ('dom', 'sub')), may hold values from -3 to 3
- restrict1: bfloat16 [30, 30, 32768], P(None, None, ('dom', 'sub')), may hold values from -1 to 1
- neighbour: int32 [6, 32768], P(None, ('dom', 'sub')), may hold values from 0 to 319
- face_slot: int32 [6, 32768], P(None, ('dom', 'sub')), may hold values from 0 to 7
- agg_map: int32 [32768], P(('dom', 'sub')), may hold values from 0 to 15, as said below
- send_list: int32 [6, 8192], P(None, ('dom', 'sub')), may hold values from 0 to 127
- restrict2: float32 [30, 30, 4096], P(None, None, ('dom', 'sub')), may hold values from -0.5 to 0.5
- coarse_nbr: int32 [8, 4096], P(None, ('dom', 'sub')), may hold values from 0 to 63
- agg2_map: int32 [4096], P(('dom', 'sub')), may hold values from 0 to 7, as said below
- coarse_slot: int32 [8, 4096], P(None, ('dom', 'sub')), may hold values from 0 to 7
Outputs:
- coarse_one: float32 [8, 30, 30, 4096], P(None, None, None, ('dom', 'sub'))
- coarse_two: float32 [8, 30, 30, 512], P(None, None, None, ('dom', 'sub'))
Inputs may be any that keep to these rules, and one draw needn't show every extreme that they name: `neighbour`: positions below 128 name the device's own elements; position 128 + r * 32 + h names entry h of the list that the partition at offset o_r sends. `agg_map`: on each device every value is taken by exactly 8 elements. `send_list`: indices of the device's own elements. `coarse_nbr`: index among the subgroup's first-level agglomerates, in device order. `agg2_map`: within each subgroup every value is taken by exactly 8 first-level agglomerates.
All inputs are finite; a program needn't handle non-finite values.
Results may differ from a plain program's by a relative error of at most 0.0029.
Values may be sent and summed in bfloat16 or wider, within the bound.
A program may use at most 128 MiB of HBM per device.

v0:
```python
import functools

import jax
import jax.numpy as jnp
from jax import lax
from jax.experimental import pallas as pl
from jax.experimental.pallas import tpu as pltpu
from jax.sharding import PartitionSpec as P

NB = 30
PAD = 32
PITCH = 40
LANES = 128
FACES = 6
SLOTS = 8
HALO = 32
REACH = 3
PEERS = 6
GROUPS = 4
ROWS = NB * PAD
QUARTER = ROWS // GROUPS
AGGS = 16
SUBS = 4
F32 = jnp.float32
BF16 = jnp.bfloat16
MESH = pl.DeviceIdType.MESH
OFFSETS = tuple(r - REACH if r < REACH else r - REACH + 1 for r in range(PEERS))


def iota(shape, dim):
    return lax.broadcasted_iota(jnp.int32, shape, dim)


def dot(a, b):
    return jnp.dot(a, b, preferred_element_type=F32)


def split(x):
    high = x.astype(BF16)
    return high, (x - high.astype(F32)).astype(BF16)


def turn_maps(restrict_ref, wide_ref, turned_ref):
    wide_ref[pl.ds(NB * PITCH, 2 * PITCH), :] = jnp.zeros((2 * PITCH, LANES), F32)
    for n in range(NB):
        wide_ref[pl.ds(n * PITCH, NB), :] = restrict_ref[n].astype(F32)
    for m in range(NB):
        turned_ref[pl.ds(m * PAD, PAD), :] = wide_ref[pl.ds(m, PAD, stride=PITCH), :].astype(BF16)


def pack_messages(turned_ref, list_ref, message_ref):
    lane_group = iota((QUARTER, LANES), 1) // HALO
    rows = turned_ref[...]
    for r in range(PEERS):
        row = list_ref[pl.ds(r, 1), :]
        four = jnp.concatenate([row] * GROUPS, axis=1)
        pick = (iota((LANES, LANES), 0) == four).astype(BF16)
        chosen = dot(rows, pick)
        packed = jnp.zeros((QUARTER, LANES), F32)
        for q in range(GROUPS):
            packed = jnp.where(lane_group == q, chosen[q * QUARTER : (q + 1) * QUARTER], packed)
        message_ref[r] = packed.astype(BF16)


def send_kernel(
    restrict_ref, list_ref, coarse_ref, turned_ref, halo_ref, maps_ref,
    wide_ref, message_ref, landed_ref, gathered_ref, send_sem, recv_sem, map_send, map_recv,
):
    dom, sub = lax.axis_index("dom"), lax.axis_index("sub")
    doms, subs = lax.axis_size("dom"), lax.axis_size("sub")
    barrier = pltpu.get_barrier_semaphore()
    for offset in OFFSETS:
        peer = lax.rem(dom + offset + doms, doms)
        pl.semaphore_signal(barrier, inc=1, device_id=(peer, sub), device_id_type=MESH)
    for step in range(1, SUBS):
        peer = lax.rem(sub + step, subs)
        pl.semaphore_signal(barrier, inc=1, device_id=(dom, peer), device_id_type=MESH)
    turn_maps(restrict_ref, wide_ref, turned_ref)
    pack_messages(turned_ref, list_ref, message_ref)
    pl.semaphore_wait(barrier, PEERS + SUBS - 1)
    copies = []
    for r, offset in enumerate(OFFSETS):
        peer = lax.rem(dom - offset + doms, doms)
        copies.append(
            pltpu.make_async_remote_copy(
                src_ref=message_ref.at[r], dst_ref=landed_ref.at[r],
                send_sem=send_sem.at[r], recv_sem=recv_sem.at[r],
                device_id=(peer, sub), device_id_type=MESH,
            )
        )
    for step in range(1, SUBS):
        peer = lax.rem(sub + step, subs)
        copies.append(
            pltpu.make_async_remote_copy(
                src_ref=coarse_ref, dst_ref=gathered_ref.at[step - 1],
                send_sem=map_send.at[step - 1], recv_sem=map_recv.at[step - 1],
                device_id=(dom, peer), device_id_type=MESH,
            )
        )
    for copy in copies:
        copy.start()
    maps_ref[0] = coarse_ref[...]
    for copy in copies:
        copy.wait()
    halo_ref[...] = landed_ref[...]
    for step in range(1, SUBS):
        maps_ref[step] = gathered_ref[step - 1]


def send_call(restrict1, send_list, coarse_pack):
    vmem = pl.BlockSpec(memory_space=pltpu.VMEM)
    return pl.pallas_call(
        send_kernel,
        name="send",
        out_shape=(
            jax.ShapeDtypeStruct((ROWS, LANES), BF16),
            jax.ShapeDtypeStruct((PEERS, QUARTER, LANES), BF16),
            jax.ShapeDtypeStruct((SUBS, LANES, LANES), F32),
        ),
        in_specs=[vmem] * 3,
        out_specs=(vmem,) * 3,
        scratch_shapes=[
            pltpu.VMEM((PAD * PITCH, LANES), F32),
            pltpu.VMEM((PEERS, QUARTER, LANES), BF16),
            pltpu.VMEM((PEERS, QUARTER, LANES), BF16),
            pltpu.VMEM((SUBS - 1, LANES, LANES), F32),
            pltpu.SemaphoreType.DMA((PEERS,)),
            pltpu.SemaphoreType.DMA((PEERS,)),
            pltpu.SemaphoreType.DMA((SUBS - 1,)),
            pltpu.SemaphoreType.DMA((SUBS - 1,)),
        ],
        compiler_params=pltpu.CompilerParams(collective_id=0, has_side_effects=True),
    )(restrict1, send_list, coarse_pack)


def main_kernel(
    turned_ref, halo_ref, maps_ref, face_ref, diag_ref, link_ref, slot_ref, group_ref,
    level_ref, owner_ref, far_ref, place_ref,
    one_ref, two_ref,
    wide_ref, near_ref, half_ref, mask_ref, member_ref, left_ref, right_ref,
    coarse_ref, high_ref, low_ref, band_ref, block_high, block_low, mixed_ref,
):
    def widen(k, carry):
        for i in range(NB):
            wide_ref[k, i, pl.ds(0, NB), :] = face_ref[k, i].astype(F32)
        return carry

    lax.fori_loop(0, FACES, widen, 0)
    for i in range(NB):
        wide_ref[FACES, i, pl.ds(0, NB), :] = diag_ref[i].astype(F32)
    near_ref[FACES] = turned_ref[...].astype(F32)

    links = jnp.concatenate([link_ref[pl.ds(k, 1), :] for k in range(FACES)], axis=1)
    pick = (iota((3 * LANES, FACES * LANES), 0) == links).astype(BF16)
    source = iota((PEERS * LANES, 2 * LANES), 0)
    target = iota((PEERS * LANES, 2 * LANES), 1)
    landing = (source // LANES) * HALO + source % HALO == target
    letters = jnp.concatenate([halo_ref[r] for r in range(PEERS)], axis=1)
    for q in range(GROUPS):
        unpack = (landing & ((source % LANES) // HALO == q)).astype(BF16)
        far = dot(letters, unpack).astype(BF16)
        rows = jnp.concatenate([turned_ref[pl.ds(q * QUARTER, QUARTER), :], far], axis=1)
        found = dot(rows, pick)
        for k in range(FACES):
            near_ref[k, pl.ds(q * QUARTER, QUARTER), :] = found[:, k * LANES : (k + 1) * LANES]

    block = 5
    blocks = NB // block

    def product(step, carry):
        k = step // blocks
        first = (step % blocks) * block
        total = [[None] * 4 for _ in range(block)]
        for m in range(NB):
            tiles = [near_ref[k, pl.ds(m * PAD + 8 * t, 8), :] for t in range(4)]
            for i in range(block):
                row = wide_ref[k, first + i, pl.ds(m, 8, stride=0), :]
                for t in range(4):
                    term = row * tiles[t]
                    total[i][t] = term if m == 0 else total[i][t] + term
        for i in range(block):
            half_ref[k, first + i] = jnp.concatenate(total[i], axis=0).astype(BF16)
        return carry

    lax.fori_loop(0, (FACES + 1) * blocks, product, 0)

    for k in range(FACES):
        row = jnp.broadcast_to(slot_ref[pl.ds(k, 1), :], (16, LANES))
        for j in range(SLOTS):
            mask_ref[k * SLOTS + j] = jnp.where(row == j, 1.0, 0.0).astype(BF16)
    group = jnp.broadcast_to(group_ref[...], (16, LANES))
    for g in range(AGGS):
        member_ref[g] = jnp.where(group == g, 1.0, 0.0).astype(BF16)

    def gather_slots(i, carry):
        column = pl.ds(pl.multiple_of(i * LANES, LANES), LANES)
        for part in range(2):
            span = pl.ds(16 * part, 16)
            half = [half_ref[k, i, span, :] for k in range(FACES + 1)]
            for j in range(SLOTS):
                total = half[0] * mask_ref[j]
                for k in range(1, FACES):
                    total = total + half[k] * mask_ref[k * SLOTS + j]
                if j == 0:
                    total = total + half[FACES]
                right_ref[pl.ds(j * PAD + 16 * part, 16), column] = total
            tile = turned_ref[pl.ds(pl.multiple_of(i * PAD, PAD) + 16 * part, 16), :]
            for g in range(AGGS):
                left_ref[pl.ds(g * PAD + 16 * part, 16), column] = tile * member_ref[g]
        return carry

    lax.fori_loop(0, NB, gather_slots, 0)
    coarse_ref[...] = lax.dot_general(
        left_ref[...], right_ref[...], (((1,), (1,)), ((), ())), preferred_element_type=F32
    )
    for g in range(AGGS):
        for j in range(SLOTS):
            one_ref[j, pl.ds(g, NB, stride=AGGS), :] = coarse_ref[
                pl.ds(g * PAD, NB), pl.ds(j * PAD, NB)
            ]

    from_lane = iota((LANES, 2 * LANES), 0)
    to_lane = iota((LANES, 2 * LANES), 1)
    for q in range(GROUPS):
        spread = ((from_lane // PAD == q) & (from_lane % PAD == to_lane % PAD)).astype(BF16)
        for s in range(SUBS):
            high, low = split(maps_ref[s])
            rows = pl.ds((s * GROUPS + q) * LANES, LANES)
            high_ref[rows, :] = dot(high, spread).astype(BF16)
            low_ref[rows, :] = dot(low, spread).astype(BF16)
    band = iota((PAD, 2 * LANES), 1) // PAD
    for t in range(SLOTS):
        band_ref[t] = jnp.where(band == t, 1.0, 0.0).astype(BF16)
    sub = lax.axis_index("sub")

    def apply_maps(g, carry):
        for j in range(SLOTS):
            far = far_ref[j, g]
            owner = lax.rem(sub - far // AGGS + SUBS, SUBS)
            rows = pl.ds(pl.multiple_of((owner * AGGS + far % AGGS) * PAD, PAD), PAD)
            band = band_ref[place_ref[j, g]]
            block_high[pl.ds(j * PAD, PAD), :] = high_ref[rows, :] * band
            block_low[pl.ds(j * PAD, PAD), :] = low_ref[rows, :] * band
        rows = pl.ds(pl.multiple_of(g * PAD, PAD), PAD)
        high, low = split(coarse_ref[rows, :])
        both = dot(jnp.concatenate([high, low], axis=0), block_high[...])
        mixed_ref[rows, :] = both[:PAD] + both[PAD:] + dot(high, block_low[...])
        return carry

    lax.fori_loop(0, AGGS, apply_maps, 0)
    high, low = split(level_ref[...])
    owner = owner_ref[...]
    picks = [jnp.where(owner == c, 1.0, 0.0).astype(BF16) for c in range(SLOTS)]
    left_high = jnp.concatenate([high * p for p in picks], axis=0)
    left_low = jnp.concatenate([low * p for p in picks], axis=0)
    right_high, right_low = split(mixed_ref[...])
    two_ref[...] = dot(left_high, right_high) + (dot(left_low, right_high) + dot(left_high, right_low))


def main_call(turned, halo, maps, face_block, diag_block, neighbour, face_slot, agg_map, level, owner, coarse_nbr, coarse_slot):
    vmem = pl.BlockSpec(memory_space=pltpu.VMEM)
    smem = pl.BlockSpec(memory_space=pltpu.SMEM)
    wide = 2 * LANES
    return pl.pallas_call(
        main_kernel,
        name="galerkin",
        out_shape=(
            jax.ShapeDtypeStruct((SLOTS, NB * AGGS, NB), F32),
            jax.ShapeDtypeStruct((SLOTS * PAD, wide), F32),
        ),
        in_specs=[vmem] * 10 + [smem] * 2,
        out_specs=(vmem, vmem),
        scratch_shapes=[
            pltpu.VMEM((FACES + 1, NB, PAD, LANES), F32),
            pltpu.VMEM((FACES + 1, ROWS, LANES), F32),
            pltpu.VMEM((FACES + 1, NB, PAD, LANES), BF16),
            pltpu.VMEM((FACES * SLOTS, 16, LANES), BF16),
            pltpu.VMEM((AGGS, 16, LANES), BF16),
            pltpu.VMEM((AGGS * PAD, NB * LANES), BF16),
            pltpu.VMEM((SLOTS * PAD, NB * LANES), BF16),
            pltpu.VMEM((AGGS * PAD, wide), F32),
            pltpu.VMEM((SUBS * AGGS * PAD, wide), BF16),
            pltpu.VMEM((SUBS * AGGS * PAD, wide), BF16),
            pltpu.VMEM((SLOTS, PAD, wide), BF16),
            pltpu.VMEM((SLOTS * PAD, wide), BF16),
            pltpu.VMEM((SLOTS * PAD, wide), BF16),
            pltpu.VMEM((AGGS * PAD, wide), F32),
        ],
        compiler_params=pltpu.CompilerParams(vmem_limit_bytes=56 * 2**20),
    )(turned, halo, maps, face_block, diag_block, neighbour, face_slot, agg_map, level, owner, coarse_nbr, coarse_slot)


def share_kernel(part_ref, sum_ref, landed_ref, send_sem, recv_sem):
    dom, sub = lax.axis_index("dom"), lax.axis_index("sub")
    subs = lax.axis_size("sub")
    rows = 2 * PAD
    barrier = pltpu.get_barrier_semaphore()
    for step in range(1, SUBS):
        peer = lax.rem(sub + step, subs)
        pl.semaphore_signal(barrier, inc=1, device_id=(dom, peer), device_id_type=MESH)
    pl.semaphore_wait(barrier, SUBS - 1)
    copies = []
    for step in range(1, SUBS):
        peer = lax.rem(sub + step, subs)
        copies.append(
            pltpu.make_async_remote_copy(
                src_ref=part_ref.at[pl.ds(pl.multiple_of(peer * rows, rows), rows), :],
                dst_ref=landed_ref.at[step - 1],
                send_sem=send_sem.at[step - 1], recv_sem=recv_sem.at[step - 1],
                device_id=(dom, peer), device_id_type=MESH,
            )
        )
    for copy in copies:
        copy.start()
    for copy in copies:
        copy.wait()
    own = part_ref[pl.ds(pl.multiple_of(sub * rows, rows), rows), :]
    sum_ref[...] = (own + landed_ref[0]) + (landed_ref[1] + landed_ref[2])


def share_call(part):
    vmem = pl.BlockSpec(memory_space=pltpu.VMEM)
    shape = (2 * PAD, 2 * LANES)
    return pl.pallas_call(
        share_kernel,
        name="share",
        out_shape=jax.ShapeDtypeStruct(shape, F32),
        in_specs=[vmem],
        out_specs=vmem,
        scratch_shapes=[
            pltpu.VMEM((SUBS - 1,) + shape, F32),
            pltpu.SemaphoreType.DMA((SUBS - 1,)),
            pltpu.SemaphoreType.DMA((SUBS - 1,)),
        ],
        compiler_params=pltpu.CompilerParams(collective_id=1, has_side_effects=True),
    )(part)


def pack_level(restrict2, agg2_map):
    padded = jnp.pad(restrict2, ((0, 2), (0, 2), (0, 0)))
    pack = padded.reshape(PAD, PAD, GROUPS, GROUPS).transpose(3, 1, 2, 0).reshape(LANES, LANES)
    level = padded.transpose(0, 2, 1).reshape(PAD, AGGS * PAD)
    owner = jnp.repeat(agg2_map, PAD).reshape(1, AGGS * PAD)
    return pack, level, owner


def per_device(
    diag_block, face_block, restrict1, neighbour, face_slot, agg_map,
    send_list, restrict2, coarse_nbr, agg2_map, coarse_slot,
):
    pack, level, owner = pack_level(restrict2, agg2_map)
    turned, halo, maps = send_call(restrict1, send_list, pack)
    one, part = main_call(
        turned, halo, maps, face_block, diag_block, neighbour, face_slot,
        agg_map.reshape(1, LANES), level, owner, coarse_nbr, coarse_slot,
    )
    total = share_call(part)
    one = one.reshape(SLOTS, NB, AGGS, NB).transpose(0, 1, 3, 2)
    two = total.reshape(2, PAD, SLOTS, PAD)[:, :NB, :, :NB].transpose(2, 1, 3, 0)
    return one, two


def solution(mesh):
    both = ("dom", "sub")
    placed = (
        P(None, None, both), P(None, None, None, both), P(None, None, both),
        P(None, both), P(None, both), P(both), P(None, both),
        P(None, None, both), P(None, both), P(both), P(None, both),
    )
    return jax.shard_map(
        per_device,
        mesh=mesh,
        in_specs=placed,
        out_specs=(P(None, None, None, both), P(None, None, None, both)),
        check_vma=False,
    )
```

profile of v0, /device:TPU:1, one launch (start us, length us, event | category | flops | bytes accessed | tf_op | source)
XLA Modules:
  0.0 52.6 jit_solution(9416256212621365908)
XLA Ops:
  0.6 0.7 %broadcast_in_dim.3 = s32[16,32]{1,0:T(8,128)S(1)} broadcast(s32[16]{0:T(128)} %param.20), dimensions={0} | broadcast | bytes 2112 | tf_op jit(solution)/shard_map/broadcast_in_dim | solution.py:343
  1.4 0.7 %reshape_reshape.3.owner_ref = s32[1,512]{1,0:T(1,128)} reshape(s32[16,32]{1,0:T(8,128)S(1)} %broadcast_in_dim.3) | data formatting | bytes 4096 | tf_op jit(solution)/shard_map/reshape;reshape | solution.py:343
  2.0 1.0 %pad_bitcast_fusion = (f32[32,16,32]{2,1,0:T(8,128)S(1)}, f32[32,32,16]{1,2,0:T(8,128)S(1)}) fusion(f32[30,30,16]{1,2,0:T(8,128)} %param.18), kind=kLoop, calls=%fused_computation.1 | loop fusion | bytes 188672 | tf_op jit(solution)/shard_map/transpose | solution.py:342
  3.0 0.8 %reshape.25.level_ref = f32[32,512]{1,0:T(8,128)} reshape(f32[32,16,32]{2,1,0:T(8,128)S(1)} %get-tuple-element.12) | data formatting | bytes 131072 | tf_op jit(solution)/shard_map/reshape | solution.py:342
  3.8 0.2 copy.13
  3.9 0.8 %reshape.23.coarse_ref = f32[128,128]{1,0:T(8,128)} reshape(f32[4,32,4,32]{3,2,1,0:T(4,128)S(1)} %bitcast.12) | data formatting | bytes 131072 | tf_op jit(solution)/shard_map/reshape | solution.py:341
  4.7 17.7 %send.1 = (bf16[960,128]{1,0:T(8,128)(2,1)}, bf16[6,240,128]{2,1,0:T(8,128)(2,1)}, f32[4,128,128]{2,1,0:T(8,128)}) custom-call(bf16[30,30,128]{2,1,0:T(8,128)(2,1)} %restrict_ref.1, s32[6,32]{1,0:T(8,128)} %list_ref.1, f32[128,128]{1,0:T(8,128)} %reshape.23.coarse_ref), custom_call_target="tpu_custom_call" | custom-call | tf_op jit(solution)/shard_map/send/pallas_call | solution.py:112
  22.4 21.4 %galerkin.1 = (f32[8,480,30]{2,1,0:T(8,128)}, f32[256,256]{1,0:T(8,128)}) custom-call(bf16[960,128]{1,0:T(8,128)(2,1)} %get-tuple-element.7.turned_ref, bf16[6,240,128]{2,1,0:T(8,128)(2,1)} %get-tuple-element.8.halo_ref, f32[4,128,128]{2,1,0:T(8,128)} %get-tuple-element.9.maps_ref, bf16[6,30,30,128]{3,2,1,0:T(8,128)(2,1)} %face_ref.1, ...), custom_call_target="tpu_custom_call" | custom-call | tf_op jit(solution)/shard_map/galerkin/pallas_call | solution.py:264
  43.8 7.0 %share.1 = f32[64,256]{1,0:T(8,128)} custom-call(f32[256,256]{1,0:T(8,128)} %get-tuple-element.11.part_ref), custom_call_target="tpu_custom_call" | custom-call | tf_op jit(solution)/shard_map/share/pallas_call | solution.py:324
  50.8 1.0 %reshape.27 = f32[2,32,8,32]{3,2,1,0:T(8,128)S(1)} reshape(f32[64,256]{1,0:T(8,128)} %share.1) | data formatting | bytes 131072 | tf_op jit(solution)/shard_map/reshape | solution.py:359
  51.8 0.8 %copy.17 = f32[2,30,8,30]{3,0,1,2:T(2,128)} copy(f32[2,30,8,30]{3,2,1,0:T(8,128)S(1)} %slice.4) | data formatting | bytes 115200
  (1 shorter events, 0.0 us)
where the time goes:
time: 52.9 us; the launch traced here: 52.6 us
  Pallas kernels  46.1 us (87%)
  local copies, waits for them, and re-layouts  5.89 us (11%)
  between operations  0.67 us (1%)
    pallas_call x1, Pallas kernels, main_call(): pl.pallas_call(main_kernel, name='galerkin', out_shape=(jax.ShapeDtypeStr...  21.4 us
    pallas_call x1, Pallas kernels, send_call(): pl.pallas_call(send_kernel, name='send', out_shape=(jax.ShapeDtypeStruct(...  17.7 us
    pallas_call x1, Pallas kernels, share_call(): pl.pallas_call(share_kernel, name='share', out_shape=jax.ShapeDtypeStruct...  6.97 us

commit v1 on v0

v1 whole, which is shorter than its diff:
```python
import jax
import jax.numpy as jnp
from jax import lax
from jax.experimental import pallas as pl
from jax.experimental.pallas import tpu as pltpu
from jax.sharding import PartitionSpec as P

NB = 30
PAD = 32
PITCH = 40
LANES = 128
FACES = 6
SLOTS = 8
HALO = 32
REACH = 3
PEERS = 6
GROUPS = 4
ROWS = NB * PAD
QUARTER = ROWS // GROUPS
AGGS = 16
SUBS = 4
F32 = jnp.float32
BF16 = jnp.bfloat16
MESH = pl.DeviceIdType.MESH
OFFSETS = tuple(r - REACH if r < REACH else r - REACH + 1 for r in range(PEERS))


def iota(shape, dim):
    return lax.broadcasted_iota(jnp.int32, shape, dim)


def dot(a, b):
    return jnp.dot(a, b, preferred_element_type=F32)


def split(x):
    high = x.astype(BF16)
    return high, (x - high.astype(F32)).astype(BF16)


def turn_maps(restrict_ref, wide_ref, turned_ref):
    wide_ref[pl.ds(NB * PITCH, 2 * PITCH), :] = jnp.zeros((2 * PITCH, LANES), F32)
    for n in range(NB):
        wide_ref[pl.ds(n * PITCH, NB), :] = restrict_ref[n].astype(F32)
    for m in range(NB):
        turned_ref[pl.ds(m * PAD, PAD), :] = wide_ref[pl.ds(m, PAD, stride=PITCH), :].astype(BF16)


def pack_messages(turned_ref, list_ref, message_ref):
    lane_group = iota((QUARTER, LANES), 1) // HALO
    rows = turned_ref[...]
    for r in range(PEERS):
        row = list_ref[pl.ds(r, 1), :]
        four = jnp.concatenate([row] * GROUPS, axis=1)
        pick = (iota((LANES, LANES), 0) == four).astype(BF16)
        chosen = dot(rows, pick)
        packed = jnp.zeros((QUARTER, LANES), F32)
        for q in range(GROUPS):
            packed = jnp.where(lane_group == q, chosen[q * QUARTER : (q + 1) * QUARTER], packed)
        message_ref[r] = packed.astype(BF16)


def pack_level(level_ref, square_ref, pack_ref, coarse_ref):
    square_ref[...] = jnp.zeros(square_ref.shape, F32)
    square_ref[pl.ds(0, NB * AGGS), pl.ds(0, NB)] = level_ref[...]
    for low in range(GROUPS):
        pieces = [
            square_ref[pl.ds(q * GROUPS + low, PAD, stride=AGGS), :] for q in range(GROUPS)
        ]
        pack_ref[pl.ds(low * PAD, PAD), :] = jnp.concatenate(pieces, axis=1)
    coarse_ref[...] = pack_ref[...].T


def spread_maps(step, values, high_ref, low_ref):
    from_lane = iota((LANES, 2 * LANES), 0)
    to_lane = iota((LANES, 2 * LANES), 1)
    high, low = split(values)
    for q in range(GROUPS):
        spread = ((from_lane // PAD == q) & (from_lane % PAD == to_lane % PAD)).astype(BF16)
        blocks = pl.ds((step * GROUPS + q) * GROUPS, GROUPS)
        shape = (GROUPS, PAD, 2 * LANES)
        high_ref[blocks] = dot(high, spread).astype(BF16).reshape(shape)
        low_ref[blocks] = dot(low, spread).astype(BF16).reshape(shape)


def product(k, step, near_ref, wide_ref, half_ref):
    block = 5
    first = step * block
    total = [[None] * 4 for _ in range(block)]
    for m in range(NB):
        tiles = [near_ref[k, pl.ds(m * PAD + 8 * t, 8), :] for t in range(4)]
        for i in range(block):
            row = wide_ref[k, first + i, pl.ds(m, 8, stride=0), :]
            for t in range(4):
                term = row * tiles[t]
                total[i][t] = term if m == 0 else total[i][t] + term
    for i in range(block):
        half_ref[k, first + i] = jnp.concatenate(total[i], axis=0).astype(BF16)


def kernel(
    restrict_ref, diag_ref, link_ref, slot_ref, group_ref, list_ref, level_ref,
    far_ref, place_ref, owner_ref, face_hbm,
    one_hbm, two_ref,
    tall_ref, turned_ref, message_ref, landed_ref, square_ref, pack_ref, coarse_ref, gathered_ref,
    face_ref, wide_ref, near_ref, half_ref, mask_ref, member_ref, left_ref, right_ref,
    one_ref, whole_ref, high_ref, low_ref, band_ref, block_high, block_low, mixed_ref,
    spot_ref, part_ref, arrived_ref,
    face_sem, one_sem, send_sem, recv_sem, map_send, map_recv, part_send, part_recv,
):
    dom, sub = lax.axis_index("dom"), lax.axis_index("sub")
    doms, subs = lax.axis_size("dom"), lax.axis_size("sub")
    face_copy = pltpu.make_async_copy(face_hbm, face_ref, face_sem)
    face_copy.start()
    barrier = pltpu.get_barrier_semaphore()
    for offset in OFFSETS:
        peer = lax.rem(dom + offset + doms, doms)
        pl.semaphore_signal(barrier, inc=1, device_id=(peer, sub), device_id_type=MESH)
    for step in range(1, SUBS):
        peer = lax.rem(sub + step, subs)
        pl.semaphore_signal(barrier, inc=1, device_id=(dom, peer), device_id_type=MESH)

    turn_maps(restrict_ref, tall_ref, turned_ref)
    pack_messages(turned_ref, list_ref, message_ref)
    pack_level(level_ref, square_ref, pack_ref, coarse_ref)
    pl.semaphore_wait(barrier, PEERS + SUBS - 1)

    halos, maps = [], []
    for r, offset in enumerate(OFFSETS):
        peer = lax.rem(dom - offset + doms, doms)
        halos.append(
            pltpu.make_async_remote_copy(
                src_ref=message_ref.at[r], dst_ref=landed_ref.at[r],
                send_sem=send_sem.at[r], recv_sem=recv_sem.at[r],
                device_id=(peer, sub), device_id_type=MESH,
            )
        )
    for step in range(1, SUBS):
        peer = lax.rem(sub + step, subs)
        maps.append(
            pltpu.make_async_remote_copy(
                src_ref=coarse_ref, dst_ref=gathered_ref.at[step - 1],
                send_sem=map_send.at[step - 1], recv_sem=map_recv.at[step - 1],
                device_id=(dom, peer), device_id_type=MESH,
            )
        )
    for copy in halos + maps:
        copy.start()

    for i in range(NB):
        wide_ref[FACES, i, pl.ds(0, NB), :] = diag_ref[i].astype(F32)
    near_ref[FACES] = turned_ref[...].astype(F32)

    def own_product(step, carry):
        product(FACES, step, near_ref, wide_ref, half_ref)
        return carry

    lax.fori_loop(0, NB // 5, own_product, 0)

    for k in range(FACES):
        row = jnp.broadcast_to(slot_ref[pl.ds(k, 1), :], (16, LANES))
        for j in range(SLOTS):
            mask_ref[k * SLOTS + j] = jnp.where(row == j, 1.0, 0.0).astype(BF16)
    group = jnp.broadcast_to(group_ref[...], (16, LANES))
    for g in range(AGGS):
        member_ref[g] = jnp.where(group == g, 1.0, 0.0).astype(BF16)

    def mask_left(i, carry):
        column = pl.ds(pl.multiple_of(i * LANES, LANES), LANES)
        for part in range(2):
            tile = turned_ref[pl.ds(pl.multiple_of(i * PAD, PAD) + 16 * part, 16), :]
            for g in range(AGGS):
                left_ref[pl.ds(g * PAD + 16 * part, 16), column] = tile * member_ref[g]
        return carry

    lax.fori_loop(0, NB, mask_left, 0)
    face_copy.wait()

    def widen(k, carry):
        for i in range(NB):
            wide_ref[k, i, pl.ds(0, NB), :] = face_ref[k, i].astype(F32)
        return carry

    lax.fori_loop(0, FACES, widen, 0)

    band = iota((PAD, 2 * LANES), 1) // PAD
    for t in range(SLOTS):
        band_ref[t] = jnp.where(band == t, 1.0, 0.0).astype(BF16)
    lane_agg = iota((PAD, AGGS * PAD), 1) // PAD
    owner = jnp.zeros((PAD, AGGS * PAD), jnp.int32)
    for g in range(AGGS):
        owner = jnp.where(lane_agg == (g % GROUPS) * GROUPS + g // GROUPS, owner_ref[0, g], owner)
    level = jnp.concatenate([pack_ref[pl.ds(x * PAD, PAD), :] for x in range(GROUPS)], axis=1)
    for c in range(SLOTS):
        rows = pl.ds((c // 2) * 2 * PAD + c % 2, PAD, stride=2)
        picked = jnp.where(owner == c, level, 0.0)
        for x in range(GROUPS):
            spot_ref[x, rows, :] = picked[:, x * LANES : (x + 1) * LANES]
    spread_maps(0, coarse_ref[...], high_ref, low_ref)
    for copy in maps:
        copy.wait()
    for step in range(1, SUBS):
        spread_maps(step, gathered_ref[step - 1], high_ref, low_ref)

    def place_blocks(g, carry):
        for j in range(SLOTS):
            far = far_ref[j, g]
            step = lax.rem(sub - lax.div(far, AGGS) + SUBS, SUBS)
            agg = lax.rem(far, AGGS)
            index = step * AGGS + lax.rem(agg, GROUPS) * GROUPS + lax.div(agg, GROUPS)
            mask = band_ref[place_ref[j, g]]
            block_high[g, pl.ds(j * PAD, PAD), :] = high_ref[index] * mask
            block_low[g, pl.ds(j * PAD, PAD), :] = low_ref[index] * mask
        return carry

    lax.fori_loop(0, AGGS, place_blocks, 0)

    links = jnp.concatenate([link_ref[pl.ds(k, 1), :] for k in range(FACES)], axis=1)
    pick = (iota((3 * LANES, FACES * LANES), 0) == links).astype(BF16)
    source = iota((PEERS * LANES, 2 * LANES), 0)
    target = iota((PEERS * LANES, 2 * LANES), 1)
    landing = (source // LANES) * HALO + source % HALO == target
    for copy in halos:
        copy.wait()
    letters = jnp.concatenate([landed_ref[r] for r in range(PEERS)], axis=1)
    for q in range(GROUPS):
        unpack = (landing & ((source % LANES) // HALO == q)).astype(BF16)
        far = dot(letters, unpack).astype(BF16)
        rows = jnp.concatenate([turned_ref[pl.ds(q * QUARTER, QUARTER), :], far], axis=1)
        found = dot(rows, pick)
        for k in range(FACES):
            near_ref[k, pl.ds(q * QUARTER, QUARTER), :] = found[:, k * LANES : (k + 1) * LANES]

    def face_product(index, carry):
        product(index // (NB // 5), index % (NB // 5), near_ref, wide_ref, half_ref)
        return carry

    lax.fori_loop(0, FACES * (NB // 5), face_product, 0)

    def gather_slots(pair, carry):
        for i in (2 * pair, 2 * pair + 1):
            column = pl.ds(pl.multiple_of(i * LANES, LANES), LANES)
            for part in range(2):
                span = pl.ds(16 * part, 16)
                half = [half_ref[k, i, span, :] for k in range(FACES + 1)]
                for j in range(SLOTS):
                    total = half[0] * mask_ref[j]
                    for k in range(1, FACES):
                        total = total + half[k] * mask_ref[k * SLOTS + j]
                    if j == 0:
                        total = total + half[FACES]
                    right_ref[pl.ds(j * PAD + 16 * part, 16), column] = total
        return carry

    lax.fori_loop(0, NB // 2, gather_slots, 0)
    whole_ref[...] = lax.dot_general(
        left_ref[...], right_ref[...], (((1,), (1,)), ((), ())), preferred_element_type=F32
    )

    for g in range(AGGS):
        high, low = split(whole_ref[pl.ds(g * PAD, PAD), :])
        both = dot(jnp.concatenate([high, low], axis=0), block_high[g])
        rows = pl.ds(((g % GROUPS) * GROUPS + g // GROUPS) * PAD, PAD)
        mixed_ref[rows, :] = both[:PAD] + both[PAD:] + dot(high, block_low[g])
    left_high, left_low = split(jnp.concatenate([spot_ref[x] for x in range(GROUPS)], axis=1))
    right_high, right_low = split(mixed_ref[...])
    part_ref[...] = dot(left_high, right_high) + (dot(left_low, right_high) + dot(left_high, right_low))

    def lay_out(aggs):
        for g in aggs:
            for j in range(SLOTS):
                one_ref[j, pl.ds(g, NB, stride=AGGS), :] = whole_ref[
                    pl.ds(g * PAD, NB), pl.ds(j * PAD, NB)
                ]

    lay_out(range(4))
    rows = 2 * PAD
    parts = []
    for step in range(1, SUBS):
        peer = lax.rem(sub + step, subs)
        parts.append(
            pltpu.make_async_remote_copy(
                src_ref=part_ref.at[pl.ds(pl.multiple_of(peer * rows, rows), rows), :],
                dst_ref=arrived_ref.at[step - 1],
                send_sem=part_send.at[step - 1], recv_sem=part_recv.at[step - 1],
                device_id=(dom, peer), device_id_type=MESH,
            )
        )
    for copy in parts:
        copy.start()
    lay_out(range(4, AGGS))
    one_copy = pltpu.make_async_copy(one_ref, one_hbm, one_sem)
    one_copy.start()
    for copy in parts:
        copy.wait()
    own = part_ref[pl.ds(pl.multiple_of(sub * rows, rows), rows), :]
    total = (own + arrived_ref[0]) + (arrived_ref[1] + arrived_ref[2])
    for t in range(SLOTS):
        two_ref[pl.ds(t * 2 * NB, 2 * NB), :] = total[: 2 * NB, t * PAD : t * PAD + NB]
    one_copy.wait()


def fused_call(*arrays):
    vmem = pl.BlockSpec(memory_space=pltpu.VMEM)
    smem = pl.BlockSpec(memory_space=pltpu.SMEM)
    hbm = pl.BlockSpec(memory_space=pl.ANY)
    dma = pltpu.SemaphoreType.DMA
    wide = 2 * LANES
    one_shape = (SLOTS, NB * AGGS, NB)
    return pl.pallas_call(
        kernel,
        name="galerkin",
        out_shape=(
            jax.ShapeDtypeStruct(one_shape, F32),
            jax.ShapeDtypeStruct((SLOTS * 2 * NB, NB), F32),
        ),
        in_specs=[vmem] * 7 + [smem] * 3 + [hbm],
        out_specs=(hbm, vmem),
        scratch_shapes=[
            pltpu.VMEM((PAD * PITCH, LANES), F32),
            pltpu.VMEM((ROWS, LANES), BF16),
            pltpu.VMEM((PEERS, QUARTER, LANES), BF16),
            pltpu.VMEM((PEERS, QUARTER, LANES), BF16),
            pltpu.VMEM((PAD * AGGS, PAD), F32),
            pltpu.VMEM((LANES, LANES), F32),
            pltpu.VMEM((LANES, LANES), F32),
            pltpu.VMEM((SUBS - 1, LANES, LANES), F32),
            pltpu.VMEM((FACES, NB, NB, LANES), BF16),
            pltpu.VMEM((FACES + 1, NB, PAD, LANES), F32),
            pltpu.VMEM((FACES + 1, ROWS, LANES), F32),
            pltpu.VMEM((FACES + 1, NB, PAD, LANES), BF16),
            pltpu.VMEM((FACES * SLOTS, 16, LANES), BF16),
            pltpu.VMEM((AGGS, 16, LANES), BF16),
            pltpu.VMEM((AGGS * PAD, NB * LANES), BF16),
            pltpu.VMEM((SLOTS * PAD, NB * LANES), BF16),
            pltpu.VMEM(one_shape, F32),
            pltpu.VMEM((AGGS * PAD, wide), F32),
            pltpu.VMEM((SUBS * AGGS, PAD, wide), BF16),
            pltpu.VMEM((SUBS * AGGS, PAD, wide), BF16),
            pltpu.VMEM((SLOTS, PAD, wide), BF16),
            pltpu.VMEM((AGGS, SLOTS * PAD, wide), BF16),
            pltpu.VMEM((AGGS, SLOTS * PAD, wide), BF16),
            pltpu.VMEM((AGGS * PAD, wide), F32),
            pltpu.VMEM((GROUPS, SLOTS * PAD, LANES), F32),
            pltpu.VMEM((SLOTS * PAD, wide), F32),
            pltpu.VMEM((SUBS - 1, 2 * PAD, wide), F32),
            dma, dma,
            dma((PEERS,)), dma((PEERS,)),
            dma((SUBS - 1,)), dma((SUBS - 1,)),
            dma((SUBS - 1,)), dma((SUBS - 1,)),
        ],
        compiler_params=pltpu.CompilerParams(
            collective_id=0, has_side_effects=True, vmem_limit_bytes=62 * 2**20
        ),
    )(*arrays)


def per_device(
    diag_block, face_block, restrict1, neighbour, face_slot, agg_map,
    send_list, restrict2, coarse_nbr, agg2_map, coarse_slot,
):
    level = restrict2.transpose(0, 2, 1).reshape(NB * AGGS, NB)
    one, two = fused_call(
        restrict1, diag_block, neighbour, face_slot, agg_map.reshape(1, LANES), send_list, level,
        coarse_nbr, coarse_slot, agg2_map.reshape(1, AGGS), face_block,
    )
    one = one.reshape(SLOTS, NB, AGGS, NB).transpose(0, 1, 3, 2)
    two = two.reshape(SLOTS, NB, 2, NB).transpose(0, 1, 3, 2)
    return one, two


def solution(mesh):
    both = ("dom", "sub")
    placed = (
        P(None, None, both), P(None, None, None, both), P(None, None, both),
        P(None, both), P(None, both), P(both), P(None, both),
        P(None, None, both), P(None, both), P(both), P(None, both),
    )
    return jax.shard_map(
        per_device,
        mesh=mesh,
        in_specs=placed,
        out_specs=(P(None, None, None, both), P(None, None, None, both)),
        check_vma=False,
    )
```

time: 52.9 us -> 42.4 us (0.80)
  Pallas kernels: 46.1 us -> 37.9 us
  local copies, waits for them, and re-layouts: 5.89 us -> 3.68 us
    pallas_call x3 -> x1, Pallas kernels: 46.1 us -> 37.9 us  [fused_call(): pl.pallas_call(kernel, name='galerkin', out_shape=(jax.ShapeDtypeStruct(o...]
    unnamed x1 -> x4, local copies, waits for them, and re-layouts: 0.82 us -> 3.68 us
    reshape x4 -> x0, local copies, waits for them, and re-layouts: 2.69 us -> none  [the longest x2 0.97 us: pack_level(): padded.reshape(PAD, PAD, GROUPS, GROUPS).transpose(3, 1, 2, 0)]
    transpose x1 -> x0, local copies, waits for them, and re-layouts: 0.98 us -> none  [pack_level(): level = padded.transpose(0, 2, 1).reshape(PAD, AGGS * PAD)]
    broadcast_in_dim x1 -> x0, local copies, waits for them, and re-layouts: 0.73 us -> none  [pack_level(): owner = jnp.repeat(agg2_map, PAD).reshape(1, AGGS * PAD)]
    another operation x1 -> x0, local copies, waits for them, and re-layouts: 0.67 us -> none  [pack_level(): owner = jnp.repeat(agg2_map, PAD).reshape(1, AGGS * PAD)]
where the time goes in v1:
time: 42.4 us; the launch traced here: 42.2 us
  Pallas kernels  37.9 us (89%)
  local copies, waits for them, and re-layouts  3.68 us (9%)
  between operations  0.65 us (2%)
    pallas_call x1, Pallas kernels, fused_call(): pl.pallas_call(kernel, name='galerkin', out_shape=(jax.ShapeDtypeStruct(o...  37.9 us
    unnamed x4, local copies, waits for them, and re-layouts  3.68 us

profile of v1, /device:TPU:1, one launch (start us, length us, event | category | flops | bytes accessed | tf_op | source)
XLA Modules:
  0.0 42.2 jit_solution(1819583197726326210)
XLA Ops:
  0.6 37.9 %galerkin.1 = (f32[8,480,30]{2,1,0:T(8,128)}, f32[480,30]{1,0:T(8,128)}) custom-call(bf16[30,30,128]{2,1,0:T(8,128)(2,1)} %restrict_ref.1, bf16[30,30,128]{2,1,0:T(8,128)(2,1)} %diag_ref.1, s32[6,128]{1,0:T(8,128)} %link_ref.1, s32[6,128]{1,0:T(8,128)} %slot_ref.1, s32[1,128]{1,0:T(1,128)} %bitcast.14, s32[6,32]{1,0:T(8,128)} %list_ref.1, ...), custom_call_target="tpu_custom_call" | custom-call | tf_op jit(solution)/shard_map/galerkin/pallas_call | solution.py:310
  38.5 0.0 copy-start
  38.5 3.0 %copy.15 = f32[8,30,30,16]{2,3,1,0:T(8,128)} copy(f32[8,30,30,16]{2,3,1,0:T(8,128)} %bitcast.11) | data formatting | bytes 921600
  41.5 0.0 copy-done
  41.5 0.7 %copy.16 = f32[8,30,30,2]{2,3,1,0:T(2,128)} copy(f32[8,30,30,2]{2,3,1,0:T(2,128)S(1)} %bitcast.12) | data formatting | bytes 115200
Async XLA Ops:
  38.5 3.0 %copy-start = (f32[480,30]{1,0:T(8,128)S(1)}, f32[480,30]{1,0:T(8,128)}, u32[]{:S(2)}) copy-start(f32[480,30]{1,0:T(8,128)} %get-tuple-element.5) | copy-start | bytes 172804

commit v2 on v1

--- a/solution.py
+++ b/solution.py
@@ -88,7 +88,7 @@
     first = step * block
     total = [[None] * 4 for _ in range(block)]
     for m in range(NB):
-        tiles = [near_ref[k, pl.ds(m * PAD + 8 * t, 8), :] for t in range(4)]
+        tiles = [near_ref[pl.ds(m * PAD + 8 * t, 8), :] for t in range(4)]
         for i in range(block):
             row = wide_ref[k, first + i, pl.ds(m, 8, stride=0), :]
             for t in range(4):
@@ -99,19 +99,19 @@
 
 
 def kernel(
+    restrict_hbm, diag_hbm, link_hbm, slot_hbm, group_hbm, list_hbm, level_hbm,
+    far_hbm, place_hbm, owner_hbm, face_hbm,
+    one_ref, two_ref,
     restrict_ref, diag_ref, link_ref, slot_ref, group_ref, list_ref, level_ref,
-    far_ref, place_ref, owner_ref, face_hbm,
-    one_hbm, two_ref,
+    far_ref, place_ref, owner_ref,
     tall_ref, turned_ref, message_ref, landed_ref, square_ref, pack_ref, coarse_ref, gathered_ref,
-    face_ref, wide_ref, near_ref, half_ref, mask_ref, member_ref, left_ref, right_ref,
-    one_ref, whole_ref, high_ref, low_ref, band_ref, block_high, block_low, mixed_ref,
-    spot_ref, part_ref, arrived_ref,
-    face_sem, one_sem, send_sem, recv_sem, map_send, map_recv, part_send, part_recv,
+    face_ref, wide_ref, near_even, near_odd, half_ref, mask_ref, member_ref, left_ref, right_ref,
+    pick_ref, unpack_ref, extended_ref, whole_ref, high_ref, low_ref, band_ref, block_high, block_low, mixed_ref,
+    spot_ref, part_ref, small_ref, arrived_ref,
+    load_sem, send_sem, recv_sem, map_send, map_recv, part_send, part_recv,
 ):
     dom, sub = lax.axis_index("dom"), lax.axis_index("sub")
     doms, subs = lax.axis_size("dom"), lax.axis_size("sub")
-    face_copy = pltpu.make_async_copy(face_hbm, face_ref, face_sem)
-    face_copy.start()
     barrier = pltpu.get_barrier_semaphore()
     for offset in OFFSETS:
         peer = lax.rem(dom + offset + doms, doms)
@@ -120,9 +120,23 @@
         peer = lax.rem(sub + step, subs)
         pl.semaphore_signal(barrier, inc=1, device_id=(dom, peer), device_id_type=MESH)
 
+    loads = [
+        pltpu.make_async_copy(source, target, load_sem.at[x])
+        for x, (source, target) in enumerate(
+            (
+                (restrict_hbm, restrict_ref), (list_hbm, list_ref), (level_hbm, level_ref),
+                (diag_hbm, diag_ref), (link_hbm, link_ref), (slot_hbm, slot_ref),
+                (group_hbm, group_ref), (owner_hbm, owner_ref), (far_hbm, far_ref),
+                (place_hbm, place_ref), (face_hbm, face_ref),
+            )
+        )
+    ]
+    for load in loads:
+        load.start()
+    loads[0].wait()
     turn_maps(restrict_ref, tall_ref, turned_ref)
+    loads[1].wait()
     pack_messages(turned_ref, list_ref, message_ref)
-    pack_level(level_ref, square_ref, pack_ref, coarse_ref)
     pl.semaphore_wait(barrier, PEERS + SUBS - 1)
 
     halos, maps = [], []
@@ -144,18 +158,24 @@
                 device_id=(dom, peer), device_id_type=MESH,
             )
         )
-    for copy in halos + maps:
+    for copy in halos:
         copy.start()
-
+    loads[2].wait()
+    pack_level(level_ref, square_ref, pack_ref, coarse_ref)
+
+    for load in loads[3:10]:
+        load.wait()
     for i in range(NB):
         wide_ref[FACES, i, pl.ds(0, NB), :] = diag_ref[i].astype(F32)
-    near_ref[FACES] = turned_ref[...].astype(F32)
+    near_odd[...] = turned_ref[...].astype(F32)
 
     def own_product(step, carry):
-        product(FACES, step, near_ref, wide_ref, half_ref)
+        product(FACES, step, near_odd, wide_ref, half_ref)
         return carry
 
     lax.fori_loop(0, NB // 5, own_product, 0)
+    for copy in maps:
+        copy.start()
 
     for k in range(FACES):
         row = jnp.broadcast_to(slot_ref[pl.ds(k, 1), :], (16, LANES))
@@ -174,7 +194,7 @@
         return carry
 
     lax.fori_loop(0, NB, mask_left, 0)
-    face_copy.wait()
+    loads[10].wait()
 
     def widen(k, carry):
         for i in range(NB):
@@ -215,27 +235,35 @@
 
     lax.fori_loop(0, AGGS, place_blocks, 0)
 
-    links = jnp.concatenate([link_ref[pl.ds(k, 1), :] for k in range(FACES)], axis=1)
-    pick = (iota((3 * LANES, FACES * LANES), 0) == links).astype(BF16)
+    for k in range(FACES):
+        pick_ref[k] = (iota((3 * LANES, LANES), 0) == link_ref[pl.ds(k, 1), :]).astype(BF16)
     source = iota((PEERS * LANES, 2 * LANES), 0)
     target = iota((PEERS * LANES, 2 * LANES), 1)
     landing = (source // LANES) * HALO + source % HALO == target
+    for q in range(GROUPS):
+        unpack_ref[q] = (landing & ((source % LANES) // HALO == q)).astype(BF16)
+    extended_ref[:, pl.ds(0, LANES)] = turned_ref[...]
     for copy in halos:
         copy.wait()
+
     letters = jnp.concatenate([landed_ref[r] for r in range(PEERS)], axis=1)
     for q in range(GROUPS):
-        unpack = (landing & ((source % LANES) // HALO == q)).astype(BF16)
-        far = dot(letters, unpack).astype(BF16)
-        rows = jnp.concatenate([turned_ref[pl.ds(q * QUARTER, QUARTER), :], far], axis=1)
-        found = dot(rows, pick)
-        for k in range(FACES):
-            near_ref[k, pl.ds(q * QUARTER, QUARTER), :] = found[:, k * LANES : (k + 1) * LANES]
-
-    def face_product(index, carry):
-        product(index // (NB // 5), index % (NB // 5), near_ref, wide_ref, half_ref)
-        return carry
-
-    lax.fori_loop(0, FACES * (NB // 5), face_product, 0)
+        far = dot(letters, unpack_ref[q]).astype(BF16)
+        extended_ref[pl.ds(q * QUARTER, QUARTER), pl.ds(LANES, 2 * LANES)] = far
+    near_even[...] = dot(extended_ref[...], pick_ref[0])
+
+    steps = NB // 5
+    for k in range(FACES):
+        now, later = (near_even, near_odd) if k % 2 == 0 else (near_odd, near_even)
+
+        def face_product(step, carry, k=k, now=now, later=later):
+            if k + 1 < FACES:
+                rows = pl.ds(pl.multiple_of(step * 5 * PAD, 5 * PAD), 5 * PAD)
+                later[rows, :] = dot(extended_ref[rows, :], pick_ref[k + 1])
+            product(k, step, now, wide_ref, half_ref)
+            return carry
+
+        lax.fori_loop(0, steps, face_product, 0)
 
     def gather_slots(pair, carry):
         for i in (2 * pair, 2 * pair + 1):
@@ -264,7 +292,9 @@
         mixed_ref[rows, :] = both[:PAD] + both[PAD:] + dot(high, block_low[g])
     left_high, left_low = split(jnp.concatenate([spot_ref[x] for x in range(GROUPS)], axis=1))
     right_high, right_low = split(mixed_ref[...])
-    part_ref[...] = dot(left_high, right_high) + (dot(left_low, right_high) + dot(left_high, right_low))
+    part = dot(left_high, right_high) + (dot(left_low, right_high) + dot(left_high, right_low))
+    part_ref[...] = part
+    small_ref[...] = part.astype(BF16)
 
     def lay_out(aggs):
         for g in aggs:
@@ -280,7 +310,7 @@
         peer = lax.rem(sub + step, subs)
         parts.append(
             pltpu.make_async_remote_copy(
-                src_ref=part_ref.at[pl.ds(pl.multiple_of(peer * rows, rows), rows), :],
+                src_ref=small_ref.at[pl.ds(pl.multiple_of(peer * rows, rows), rows), :],
                 dst_ref=arrived_ref.at[step - 1],
                 send_sem=part_send.at[step - 1], recv_sem=part_recv.at[step - 1],
                 device_id=(dom, peer), device_id_type=MESH,
@@ -289,21 +319,18 @@
     for copy in parts:
         copy.start()
     lay_out(range(4, AGGS))
-    one_copy = pltpu.make_async_copy(one_ref, one_hbm, one_sem)
-    one_copy.start()
     for copy in parts:
         copy.wait()
     own = part_ref[pl.ds(pl.multiple_of(sub * rows, rows), rows), :]
-    total = (own + arrived_ref[0]) + (arrived_ref[1] + arrived_ref[2])
+    others = [arrived_ref[x].astype(F32) for x in range(SUBS - 1)]
+    total = (own + others[0]) + (others[1] + others[2])
     for t in range(SLOTS):
         two_ref[pl.ds(t * 2 * NB, 2 * NB), :] = total[: 2 * NB, t * PAD : t * PAD + NB]
-    one_copy.wait()
 
 
 def fused_call(*arrays):
     vmem = pl.BlockSpec(memory_space=pltpu.VMEM)
-    smem = pl.BlockSpec(memory_space=pltpu.SMEM)
-    hbm = pl.BlockSpec(memory_space=pl.ANY)
+    hbm = pl.BlockSpec(memory_space=pltpu.HBM)
     dma = pltpu.SemaphoreType.DMA
     wide = 2 * LANES
     one_shape = (SLOTS, NB * AGGS, NB)
@@ -314,9 +341,19 @@
             jax.ShapeDtypeStruct(one_shape, F32),
             jax.ShapeDtypeStruct((SLOTS * 2 * NB, NB), F32),
         ),
-        in_specs=[vmem] * 7 + [smem] * 3 + [hbm],
-        out_specs=(hbm, vmem),
+        in_specs=[hbm] * 11,
+        out_specs=(vmem, vmem),
         scratch_shapes=[
+            pltpu.VMEM((NB, NB, LANES), BF16),
+            pltpu.VMEM((NB, NB, LANES), BF16),
+            pltpu.VMEM((FACES, LANES), jnp.int32),
+            pltpu.VMEM((FACES, LANES), jnp.int32),
+            pltpu.VMEM((1, LANES), jnp.int32),
+            pltpu.VMEM((PEERS, HALO), jnp.int32),
+            pltpu.VMEM((NB * AGGS, NB), F32),
+            pltpu.SMEM((SLOTS, AGGS), jnp.int32),
+            pltpu.SMEM((SLOTS, AGGS), jnp.int32),
+            pltpu.SMEM((1, AGGS), jnp.int32),
             pltpu.VMEM((PAD * PITCH, LANES), F32),
             pltpu.VMEM((ROWS, LANES), BF16),
             pltpu.VMEM((PEERS, QUARTER, LANES), BF16),
@@ -327,13 +364,16 @@
             pltpu.VMEM((SUBS - 1, LANES, LANES), F32),
             pltpu.VMEM((FACES, NB, NB, LANES), BF16),
             pltpu.VMEM((FACES + 1, NB, PAD, LANES), F32),
-            pltpu.VMEM((FACES + 1, ROWS, LANES), F32),
+            pltpu.VMEM((ROWS, LANES), F32),
+            pltpu.VMEM((ROWS, LANES), F32),
             pltpu.VMEM((FACES + 1, NB, PAD, LANES), BF16),
             pltpu.VMEM((FACES * SLOTS, 16, LANES), BF16),
             pltpu.VMEM((AGGS, 16, LANES), BF16),
             pltpu.VMEM((AGGS * PAD, NB * LANES), BF16),
             pltpu.VMEM((SLOTS * PAD, NB * LANES), BF16),
-            pltpu.VMEM(one_shape, F32),
+            pltpu.VMEM((FACES, 3 * LANES, LANES), BF16),
+            pltpu.VMEM((GROUPS, PEERS * LANES, wide), BF16),
+            pltpu.VMEM((ROWS, 3 * LANES), BF16),
             pltpu.VMEM((AGGS * PAD, wide), F32),
             pltpu.VMEM((SUBS * AGGS, PAD, wide), BF16),
             pltpu.VMEM((SUBS * AGGS, PAD, wide), BF16),
@@ -343,16 +383,17 @@
             pltpu.VMEM((AGGS * PAD, wide), F32),
             pltpu.VMEM((GROUPS, SLOTS * PAD, LANES), F32),
             pltpu.VMEM((SLOTS * PAD, wide), F32),
-            pltpu.VMEM((SUBS - 1, 2 * PAD, wide), F32),
-            dma, dma,
+            pltpu.VMEM((SLOTS * PAD, wide), BF16),
+            pltpu.VMEM((SUBS - 1, 2 * PAD, wide), BF16),
+            dma((11,)),
             dma((PEERS,)), dma((PEERS,)),
             dma((SUBS - 1,)), dma((SUBS - 1,)),
             dma((SUBS - 1,)), dma((SUBS - 1,)),
         ],
         compiler_params=pltpu.CompilerParams(
-            collective_id=0, has_side_effects=True, vmem_limit_bytes=62 * 2**20
+            collective_id=0, has_side_effects=True, vmem_limit_bytes=42 * 2**20
         ),
-    )(*arrays)
+    )(*[pltpu.with_memory_space_constraint(a, pltpu.HBM) for a in arrays])
 
 
 def per_device(

time: 42.4 us -> 39 us (0.920)
  local copies, waits for them, and re-layouts: 3.68 us -> 1.97 us
  Pallas kernels: 37.9 us -> 36.3 us
    unnamed x4 -> x2, local copies, waits for them, and re-layouts: 3.68 us -> 1.97 us
    pallas_call x1, Pallas kernels: 37.9 us -> 36.3 us  [fused_call(): pl.pallas_call(kernel, name='galerkin', out_shape=(jax.ShapeDtypeStruct(o...]
where the time goes in v2:
time: 39 us; the launch traced here: 38.9 us
  Pallas kernels  36.3 us (93%)
  local copies, waits for them, and re-layouts  1.97 us (5%)
  between operations  0.64 us (2%)
    pallas_call x1, Pallas kernels, fused_call(): pl.pallas_call(kernel, name='galerkin', out_shape=(jax.ShapeDtypeStruct(o...  36.3 us
    unnamed x2, local copies, waits for them, and re-layouts  1.97 us

profile of v2, /device:TPU:1, one launch (start us, length us, event | category | flops | bytes accessed | tf_op | source)
XLA Modules:
  0.0 38.9 jit_solution(3747628501233244168)
XLA Ops:
  0.6 36.3 %galerkin.1 = (f32[8,480,30]{2,1,0:T(8,128)S(1)}, f32[480,30]{1,0:T(8,128)S(1)}) custom-call(bf16[30,30,128]{2,1,0:T(8,128)(2,1)} %restrict_hbm.1, bf16[30,30,128]{2,1,0:T(8,128)(2,1)} %diag_hbm.1, s32[6,128]{1,0:T(8,128)} %link_hbm.1, s32[6,128]{1,0:T(8,128)} %slot_hbm.1, s32[1,128]{1,0:T(1,128)} %bitcast.14, s32[6,32]{1,0:T(8,128)} %list_hbm.1, ...), custom_call_target="tpu_custom_call" | custom-call | tf_op jit(solution)/shard_map/galerkin/pallas_call | solution.py:337
  36.9 1.3 %copy.15 = f32[8,30,30,16]{2,3,1,0:T(8,128)} copy(f32[8,30,30,16]{2,3,1,0:T(8,128)S(1)} %bitcast.11) | data formatting | bytes 921600
  38.2 0.7 %copy.16 = f32[8,30,30,2]{2,3,1,0:T(2,128)} copy(f32[8,30,30,2]{2,3,1,0:T(2,128)S(1)} %bitcast.12) | data formatting | bytes 115200

commit v3 on v2

--- a/solution.py
+++ b/solution.py
@@ -46,18 +46,16 @@
         turned_ref[pl.ds(m * PAD, PAD), :] = wide_ref[pl.ds(m, PAD, stride=PITCH), :].astype(BF16)
 
 
-def pack_messages(turned_ref, list_ref, message_ref):
+def pack_message(r, turned_ref, list_ref, message_ref):
     lane_group = iota((QUARTER, LANES), 1) // HALO
-    rows = turned_ref[...]
-    for r in range(PEERS):
-        row = list_ref[pl.ds(r, 1), :]
-        four = jnp.concatenate([row] * GROUPS, axis=1)
-        pick = (iota((LANES, LANES), 0) == four).astype(BF16)
-        chosen = dot(rows, pick)
-        packed = jnp.zeros((QUARTER, LANES), F32)
-        for q in range(GROUPS):
-            packed = jnp.where(lane_group == q, chosen[q * QUARTER : (q + 1) * QUARTER], packed)
-        message_ref[r] = packed.astype(BF16)
+    row = list_ref[pl.ds(r, 1), :]
+    four = jnp.concatenate([row] * GROUPS, axis=1)
+    pick = (iota((LANES, LANES), 0) == four).astype(BF16)
+    chosen = dot(turned_ref[...], pick)
+    packed = chosen[:QUARTER]
+    for q in range(1, GROUPS):
+        packed = jnp.where(lane_group == q, chosen[q * QUARTER : (q + 1) * QUARTER], packed)
+    message_ref[r] = packed.astype(BF16)
 
 
 def pack_level(level_ref, square_ref, pack_ref, coarse_ref):
@@ -83,19 +81,21 @@
         low_ref[blocks] = dot(low, spread).astype(BF16).reshape(shape)
 
 
-def product(k, step, near_ref, wide_ref, half_ref):
+def product(k, ten, part, near_ref, wide_ref, half_ref):
     block = 5
-    first = step * block
     total = [[None] * 4 for _ in range(block)]
     for m in range(NB):
         tiles = [near_ref[pl.ds(m * PAD + 8 * t, 8), :] for t in range(4)]
         for i in range(block):
-            row = wide_ref[k, first + i, pl.ds(m, 8, stride=0), :]
+            row = wide_ref[k, ten * 10 + part * block + i, pl.ds(m, 8, stride=0), :]
             for t in range(4):
                 term = row * tiles[t]
                 total[i][t] = term if m == 0 else total[i][t] + term
     for i in range(block):
-        half_ref[k, first + i] = jnp.concatenate(total[i], axis=0).astype(BF16)
+        pair, side = divmod(part * block + i, 2)
+        half_ref[k, ten * 5 + pair, :, pl.ds(side * LANES, LANES)] = jnp.concatenate(
+            total[i], axis=0
+        ).astype(BF16)
 
 
 def kernel(
@@ -112,14 +112,6 @@
 ):
     dom, sub = lax.axis_index("dom"), lax.axis_index("sub")
     doms, subs = lax.axis_size("dom"), lax.axis_size("sub")
-    barrier = pltpu.get_barrier_semaphore()
-    for offset in OFFSETS:
-        peer = lax.rem(dom + offset + doms, doms)
-        pl.semaphore_signal(barrier, inc=1, device_id=(peer, sub), device_id_type=MESH)
-    for step in range(1, SUBS):
-        peer = lax.rem(sub + step, subs)
-        pl.semaphore_signal(barrier, inc=1, device_id=(dom, peer), device_id_type=MESH)
-
     loads = [
         pltpu.make_async_copy(source, target, load_sem.at[x])
         for x, (source, target) in enumerate(
@@ -131,13 +123,21 @@
             )
         )
     ]
-    for load in loads:
+    for load in loads[:3]:
+        load.start()
+    barrier = pltpu.get_barrier_semaphore()
+    for offset in OFFSETS:
+        peer = lax.rem(dom + offset + doms, doms)
+        pl.semaphore_signal(barrier, inc=1, device_id=(peer, sub), device_id_type=MESH)
+    for step in range(1, SUBS):
+        peer = lax.rem(sub + step, subs)
+        pl.semaphore_signal(barrier, inc=1, device_id=(dom, peer), device_id_type=MESH)
+
+    for load in loads[3:]:
         load.start()
     loads[0].wait()
     turn_maps(restrict_ref, tall_ref, turned_ref)
     loads[1].wait()
-    pack_messages(turned_ref, list_ref, message_ref)
-    pl.semaphore_wait(barrier, PEERS + SUBS - 1)
 
     halos, maps = [], []
     for r, offset in enumerate(OFFSETS):
@@ -158,8 +158,11 @@
                 device_id=(dom, peer), device_id_type=MESH,
             )
         )
-    for copy in halos:
-        copy.start()
+    for r in range(PEERS):
+        pack_message(r, turned_ref, list_ref, message_ref)
+    pl.semaphore_wait(barrier, PEERS + SUBS - 1)
+    for r in (0, 5, 1, 4, 2, 3):
+        halos[r].start()
     loads[2].wait()
     pack_level(level_ref, square_ref, pack_ref, coarse_ref)
 
@@ -170,15 +173,17 @@
     near_odd[...] = turned_ref[...].astype(F32)
 
     def own_product(step, carry):
-        product(FACES, step, near_odd, wide_ref, half_ref)
+        for part in range(2):
+            product(FACES, step, part, near_odd, wide_ref, half_ref)
         return carry
 
-    lax.fori_loop(0, NB // 5, own_product, 0)
+    lax.fori_loop(0, NB // 10, own_product, 0)
     for copy in maps:
         copy.start()
 
     for k in range(FACES):
-        row = jnp.broadcast_to(slot_ref[pl.ds(k, 1), :], (16, LANES))
+        one_row = slot_ref[pl.ds(k, 1), :]
+        row = jnp.broadcast_to(jnp.concatenate([one_row, one_row], axis=1), (8, 2 * LANES))
         for j in range(SLOTS):
             mask_ref[k * SLOTS + j] = jnp.where(row == j, 1.0, 0.0).astype(BF16)
     group = jnp.broadcast_to(group_ref[...], (16, LANES))
@@ -252,32 +257,32 @@
         extended_ref[pl.ds(q * QUARTER, QUARTER), pl.ds(LANES, 2 * LANES)] = far
     near_even[...] = dot(extended_ref[...], pick_ref[0])
 
-    steps = NB // 5
+    steps = NB // 10
     for k in range(FACES):
         now, later = (near_even, near_odd) if k % 2 == 0 else (near_odd, near_even)
 
         def face_product(step, carry, k=k, now=now, later=later):
             if k + 1 < FACES:
-                rows = pl.ds(pl.multiple_of(step * 5 * PAD, 5 * PAD), 5 * PAD)
+                rows = pl.ds(pl.multiple_of(step * 10 * PAD, 10 * PAD), 10 * PAD)
                 later[rows, :] = dot(extended_ref[rows, :], pick_ref[k + 1])
-            product(k, step, now, wide_ref, half_ref)
+            for part in range(2):
+                product(k, step, part, now, wide_ref, half_ref)
             return carry
 
         lax.fori_loop(0, steps, face_product, 0)
 
     def gather_slots(pair, carry):
-        for i in (2 * pair, 2 * pair + 1):
-            column = pl.ds(pl.multiple_of(i * LANES, LANES), LANES)
-            for part in range(2):
-                span = pl.ds(16 * part, 16)
-                half = [half_ref[k, i, span, :] for k in range(FACES + 1)]
-                for j in range(SLOTS):
-                    total = half[0] * mask_ref[j]
-                    for k in range(1, FACES):
-                        total = total + half[k] * mask_ref[k * SLOTS + j]
-                    if j == 0:
-                        total = total + half[FACES]
-                    right_ref[pl.ds(j * PAD + 16 * part, 16), column] = total
+        column = pl.ds(pl.multiple_of(pair * 2 * LANES, 2 * LANES), 2 * LANES)
+        for part in range(4):
+            span = pl.ds(8 * part, 8)
+            half = [half_ref[k, pair, span, :] for k in range(FACES + 1)]
+            for j in range(SLOTS):
+                total = half[0] * mask_ref[j]
+                for k in range(1, FACES):
+                    total = total + half[k] * mask_ref[k * SLOTS + j]
+                if j == 0:
+                    total = total + half[FACES]
+                right_ref[pl.ds(j * PAD + 8 * part, 8), column] = total
         return carry
 
     lax.fori_loop(0, NB // 2, gather_slots, 0)
@@ -366,8 +371,8 @@
             pltpu.VMEM((FACES + 1, NB, PAD, LANES), F32),
             pltpu.VMEM((ROWS, LANES), F32),
             pltpu.VMEM((ROWS, LANES), F32),
-            pltpu.VMEM((FACES + 1, NB, PAD, LANES), BF16),
-            pltpu.VMEM((FACES * SLOTS, 16, LANES), BF16),
+            pltpu.VMEM((FACES + 1, NB // 2, PAD, wide), BF16),
+            pltpu.VMEM((FACES * SLOTS, 8, wide), BF16),
             pltpu.VMEM((AGGS, 16, LANES), BF16),
             pltpu.VMEM((AGGS * PAD, NB * LANES), BF16),
             pltpu.VMEM((SLOTS * PAD, NB * LANES), BF16),

time: 39 us -> 37.5 us (0.962)
  Pallas kernels: 36.3 us -> 34.8 us
    pallas_call x1, Pallas kernels: 36.3 us -> 34.8 us  [fused_call(): pl.pallas_call(kernel, name='galerkin', out_shape=(jax.ShapeDtypeStruct(o...]
where the time goes in v3:
time: 37.5 us; the launch traced here: 37.4 us
  Pallas kernels  34.8 us (93%)
  local copies, waits for them, and re-layouts  1.97 us (5%)
  between operations  0.64 us (2%)
    pallas_call x1, Pallas kernels, fused_call(): pl.pallas_call(kernel, name='galerkin', out_shape=(jax.ShapeDtypeStruct(o...  34.8 us
    unnamed x2, local copies, waits for them, and re-layouts  1.97 us

profile of v3, /device:TPU:1, one launch (start us, length us, event | category | flops | bytes accessed | tf_op | source)
XLA Modules:
  0.0 37.4 jit_solution(17797253506696126942)
XLA Ops:
  0.6 34.8 %galerkin.1 = (f32[8,480,30]{2,1,0:T(8,128)S(1)}, f32[480,30]{1,0:T(8,128)S(1)}) custom-call(bf16[30,30,128]{2,1,0:T(8,128)(2,1)} %restrict_hbm.1, bf16[30,30,128]{2,1,0:T(8,128)(2,1)} %diag_hbm.1, s32[6,128]{1,0:T(8,128)} %link_hbm.1, s32[6,128]{1,0:T(8,128)} %slot_hbm.1, s32[1,128]{1,0:T(1,128)} %bitcast.14, s32[6,32]{1,0:T(8,128)} %list_hbm.1, ...), custom_call_target="tpu_custom_call" | custom-call | tf_op jit(solution)/shard_map/galerkin/pallas_call | solution.py:342
  35.5 1.3 %copy.15 = f32[8,30,30,16]{2,3,1,0:T(8,128)} copy(f32[8,30,30,16]{2,3,1,0:T(8,128)S(1)} %bitcast.11) | data formatting | bytes 921600
  36.8 0.7 %copy.16 = f32[8,30,30,2]{2,3,1,0:T(2,128)} copy(f32[8,30,30,2]{2,3,1,0:T(2,128)S(1)} %bitcast.12) | data formatting | bytes 115200

commit v4 on v3

--- a/solution.py
+++ b/solution.py
@@ -401,6 +401,32 @@
     )(*[pltpu.with_memory_space_constraint(a, pltpu.HBM) for a in arrays])
 
 
+def place_kernel(one_ref, two_ref, one_hbm, two_hbm, sem):
+    copies = [pltpu.make_async_copy(two_ref, two_hbm, sem.at[SLOTS])]
+    for j in range(SLOTS):
+        copies.append(pltpu.make_async_copy(one_ref.at[j], one_hbm.at[j], sem.at[j]))
+    for copy in copies:
+        copy.start()
+    for copy in copies:
+        copy.wait()
+
+
+def place_call(one, two):
+    anywhere = pl.BlockSpec(memory_space=pl.ANY)
+    return pl.pallas_call(
+        place_kernel,
+        name="place",
+        out_shape=(
+            jax.ShapeDtypeStruct(one.shape, F32),
+            jax.ShapeDtypeStruct(two.shape, F32),
+        ),
+        in_specs=[anywhere] * 2,
+        out_specs=(anywhere,) * 2,
+        scratch_shapes=[pltpu.SemaphoreType.DMA((SLOTS + 1,))],
+        compiler_params=pltpu.CompilerParams(vmem_limit_bytes=2**20),
+    )(one, two)
+
+
 def per_device(
     diag_block, face_block, restrict1, neighbour, face_slot, agg_map,
     send_list, restrict2, coarse_nbr, agg2_map, coarse_slot,
@@ -410,6 +436,7 @@
         restrict1, diag_block, neighbour, face_slot, agg_map.reshape(1, LANES), send_list, level,
         coarse_nbr, coarse_slot, agg2_map.reshape(1, AGGS), face_block,
     )
+    one, two = place_call(one, two)
     one = one.reshape(SLOTS, NB, AGGS, NB).transpose(0, 1, 3, 2)
     two = two.reshape(SLOTS, NB, 2, NB).transpose(0, 1, 3, 2)
     return one, two

time: 37.5 us -> 37 us (0.987)
  local copies, waits for them, and re-layouts: 1.97 us -> 0 us
  Pallas kernels: 34.8 us -> 36.3 us
    unnamed x2 -> x0, local copies, waits for them, and re-layouts: 1.97 us -> none
    pallas_call x0 -> x1, Pallas kernels: none -> 1.42 us  [place_call(): pl.pallas_call(place_kernel, name='place', out_shape=(jax.ShapeDtypeStruc...]
where the time goes in v4:
time: 37 us; the launch traced here: 36.9 us
  Pallas kernels  36.3 us (98%)
  between operations  0.64 us (2%)
    pallas_call x1, Pallas kernels, fused_call(): pl.pallas_call(kernel, name='galerkin', out_shape=(jax.ShapeDtypeStruct(o...  34.8 us
    pallas_call x1, Pallas kernels, place_call(): pl.pallas_call(place_kernel, name='place', out_shape=(jax.ShapeDtypeStruc...  1.42 us

profile of v4, /device:TPU:1, one launch (start us, length us, event | category | flops | bytes accessed | tf_op | source)
XLA Modules:
  0.0 36.9 jit_solution(14630804988734566079)
XLA Ops:
  0.6 34.8 %galerkin.1 = (f32[8,480,30]{2,1,0:T(8,128)S(1)}, f32[480,30]{1,0:T(8,128)S(1)}) custom-call(bf16[30,30,128]{2,1,0:T(8,128)(2,1)} %restrict_hbm.1, bf16[30,30,128]{2,1,0:T(8,128)(2,1)} %diag_hbm.1, s32[6,128]{1,0:T(8,128)} %link_hbm.1, s32[6,128]{1,0:T(8,128)} %slot_hbm.1, s32[1,128]{1,0:T(1,128)} %bitcast.12, s32[6,32]{1,0:T(8,128)} %list_hbm.1, ...), custom_call_target="tpu_custom_call" | custom-call | tf_op jit(solution)/shard_map/galerkin/pallas_call | solution.py:342
  35.5 1.4 %place.1 = (f32[8,480,30]{2,1,0:T(8,128)}, f32[480,30]{1,0:T(8,128)}) custom-call(f32[8,480,30]{2,1,0:T(8,128)S(1)} %get-tuple-element.6.one_ref, f32[480,30]{1,0:T(8,128)S(1)} %get-tuple-element.7.two_ref), custom_call_target="tpu_custom_call" | custom-call | tf_op jit(solution)/shard_map/place/pallas_call | solution.py:416

commit v5 on v4

--- a/solution.py
+++ b/solution.py
@@ -46,16 +46,18 @@
         turned_ref[pl.ds(m * PAD, PAD), :] = wide_ref[pl.ds(m, PAD, stride=PITCH), :].astype(BF16)
 
 
-def pack_message(r, turned_ref, list_ref, message_ref):
-    lane_group = iota((QUARTER, LANES), 1) // HALO
-    row = list_ref[pl.ds(r, 1), :]
-    four = jnp.concatenate([row] * GROUPS, axis=1)
-    pick = (iota((LANES, LANES), 0) == four).astype(BF16)
-    chosen = dot(turned_ref[...], pick)
-    packed = chosen[:QUARTER]
-    for q in range(1, GROUPS):
-        packed = jnp.where(lane_group == q, chosen[q * QUARTER : (q + 1) * QUARTER], packed)
-    message_ref[r] = packed.astype(BF16)
+def pack_messages(turned_ref, list_ref, message_ref):
+    groups = jnp.concatenate(
+        [turned_ref[pl.ds(q * QUARTER, QUARTER), :] for q in range(GROUPS)], axis=1
+    )
+    base = (iota((1, 2 * LANES), 1) // HALO) % GROUPS * LANES
+    for pair in ((0, 5), (1, 4), (2, 3)):
+        rows = [list_ref[pl.ds(r, 1), :] for r in pair for _ in range(GROUPS)]
+        wanted = jnp.concatenate(rows, axis=1) + base
+        pick = (iota((GROUPS * LANES, 2 * LANES), 0) == wanted).astype(BF16)
+        chosen = dot(groups, pick).astype(BF16)
+        for x, r in enumerate(pair):
+            message_ref[r] = chosen[:, x * LANES : (x + 1) * LANES]
 
 
 def pack_level(level_ref, square_ref, pack_ref, coarse_ref):
@@ -158,8 +160,7 @@
                 device_id=(dom, peer), device_id_type=MESH,
             )
         )
-    for r in range(PEERS):
-        pack_message(r, turned_ref, list_ref, message_ref)
+    pack_messages(turned_ref, list_ref, message_ref)
     pl.semaphore_wait(barrier, PEERS + SUBS - 1)
     for r in (0, 5, 1, 4, 2, 3):
         halos[r].start()
@@ -321,8 +322,8 @@
                 device_id=(dom, peer), device_id_type=MESH,
             )
         )
-    for copy in parts:
-        copy.start()
+    for step in (2, 1, 3):
+        parts[step - 1].start()
     lay_out(range(4, AGGS))
     for copy in parts:
         copy.wait()

time: 37 us -> 36.6 us (0.989)
  Pallas kernels: 36.3 us -> 35.8 us
    pallas_call x1, Pallas kernels: 34.8 us -> 34.4 us  [fused_call(): pl.pallas_call(kernel, name='galerkin', out_shape=(jax.ShapeDtypeStruct(o...]
where the time goes in v5:
time: 36.6 us; the launch traced here: 36.5 us
  Pallas kernels  35.8 us (98%)
  between operations  0.64 us (2%)
    pallas_call x1, Pallas kernels, fused_call(): pl.pallas_call(kernel, name='galerkin', out_shape=(jax.ShapeDtypeStruct(o...  34.4 us
    pallas_call x1, Pallas kernels, place_call(): pl.pallas_call(place_kernel, name='place', out_shape=(jax.ShapeDtypeStruc...  1.42 us

profile of v5, /device:TPU:1, one launch (start us, length us, event | category | flops | bytes accessed | tf_op | source)
XLA Modules:
  0.0 36.5 jit_solution(17562391308408480697)
XLA Ops:
  0.6 34.4 %galerkin.1 = (f32[8,480,30]{2,1,0:T(8,128)S(1)}, f32[480,30]{1,0:T(8,128)S(1)}) custom-call(bf16[30,30,128]{2,1,0:T(8,128)(2,1)} %restrict_hbm.1, bf16[30,30,128]{2,1,0:T(8,128)(2,1)} %diag_hbm.1, s32[6,128]{1,0:T(8,128)} %link_hbm.1, s32[6,128]{1,0:T(8,128)} %slot_hbm.1, s32[1,128]{1,0:T(1,128)} %bitcast.12, s32[6,32]{1,0:T(8,128)} %list_hbm.1, ...), custom_call_target="tpu_custom_call" | custom-call | tf_op jit(solution)/shard_map/galerkin/pallas_call | solution.py:343
  35.0 1.4 %place.1 = (f32[8,480,30]{2,1,0:T(8,128)}, f32[480,30]{1,0:T(8,128)}) custom-call(f32[8,480,30]{2,1,0:T(8,128)S(1)} %get-tuple-element.6.one_ref, f32[480,30]{1,0:T(8,128)S(1)} %get-tuple-element.7.two_ref), custom_call_target="tpu_custom_call" | custom-call | tf_op jit(solution)/shard_map/place/pallas_call | solution.py:417

commit v6 on v5

--- a/solution.py
+++ b/solution.py
@@ -178,9 +178,9 @@
             product(FACES, step, part, near_odd, wide_ref, half_ref)
         return carry
 
+    for step in (2, 1, 3):
+        maps[step - 1].start()
     lax.fori_loop(0, NB // 10, own_product, 0)
-    for copy in maps:
-        copy.start()
 
     for k in range(FACES):
         one_row = slot_ref[pl.ds(k, 1), :]
@@ -222,6 +222,14 @@
         picked = jnp.where(owner == c, level, 0.0)
         for x in range(GROUPS):
             spot_ref[x, rows, :] = picked[:, x * LANES : (x + 1) * LANES]
+    for k in range(FACES):
+        pick_ref[k] = (iota((3 * LANES, LANES), 0) == link_ref[pl.ds(k, 1), :]).astype(BF16)
+    source = iota((PEERS * LANES, 2 * LANES), 0)
+    target = iota((PEERS * LANES, 2 * LANES), 1)
+    landing = (source // LANES) * HALO + source % HALO == target
+    for q in range(GROUPS):
+        unpack_ref[q] = (landing & ((source % LANES) // HALO == q)).astype(BF16)
+    extended_ref[:, pl.ds(0, LANES)] = turned_ref[...]
     spread_maps(0, coarse_ref[...], high_ref, low_ref)
     for copy in maps:
         copy.wait()
@@ -241,14 +249,6 @@
 
     lax.fori_loop(0, AGGS, place_blocks, 0)
 
-    for k in range(FACES):
-        pick_ref[k] = (iota((3 * LANES, LANES), 0) == link_ref[pl.ds(k, 1), :]).astype(BF16)
-    source = iota((PEERS * LANES, 2 * LANES), 0)
-    target = iota((PEERS * LANES, 2 * LANES), 1)
-    landing = (source // LANES) * HALO + source % HALO == target
-    for q in range(GROUPS):
-        unpack_ref[q] = (landing & ((source % LANES) // HALO == q)).astype(BF16)
-    extended_ref[:, pl.ds(0, LANES)] = turned_ref[...]
     for copy in halos:
         copy.wait()
 

time: 36.6 us -> 35.1 us (0.959)
  Pallas kernels: 35.8 us -> 34.3 us
    pallas_call x1, Pallas kernels: 34.4 us -> 32.9 us  [fused_call(): pl.pallas_call(kernel, name='galerkin', out_shape=(jax.ShapeDtypeStruct(o...]
where the time goes in v6:
time: 35.1 us; the launch traced here: 35 us
  Pallas kernels  34.3 us (98%)
  between operations  0.64 us (2%)
    pallas_call x1, Pallas kernels, fused_call(): pl.pallas_call(kernel, name='galerkin', out_shape=(jax.ShapeDtypeStruct(o...  32.9 us
    pallas_call x1, Pallas kernels, place_call(): pl.pallas_call(place_kernel, name='place', out_shape=(jax.ShapeDtypeStruc...  1.42 us

profile of v6, /device:TPU:1, one launch (start us, length us, event | category | flops | bytes accessed | tf_op | source)
XLA Modules:
  0.0 35.0 jit_solution(9024829041899536427)
XLA Ops:
  0.6 32.9 %galerkin.1 = (f32[8,480,30]{2,1,0:T(8,128)S(1)}, f32[480,30]{1,0:T(8,128)S(1)}) custom-call(bf16[30,30,128]{2,1,0:T(8,128)(2,1)} %restrict_hbm.1, bf16[30,30,128]{2,1,0:T(8,128)(2,1)} %diag_hbm.1, s32[6,128]{1,0:T(8,128)} %link_hbm.1, s32[6,128]{1,0:T(8,128)} %slot_hbm.1, s32[1,128]{1,0:T(1,128)} %bitcast.12, s32[6,32]{1,0:T(8,128)} %list_hbm.1, ...), custom_call_target="tpu_custom_call" | custom-call | tf_op jit(solution)/shard_map/galerkin/pallas_call | solution.py:343
  33.6 1.4 %place.1 = (f32[8,480,30]{2,1,0:T(8,128)}, f32[480,30]{1,0:T(8,128)}) custom-call(f32[8,480,30]{2,1,0:T(8,128)S(1)} %get-tuple-element.6.one_ref, f32[480,30]{1,0:T(8,128)S(1)} %get-tuple-element.7.two_ref), custom_call_target="tpu_custom_call" | custom-call | tf_op jit(solution)/shard_map/place/pallas_call | solution.py:417
